TPU v7x, 256 devices: a whole 4x4x8 slice. The times are simulated.
256 devices in a mesh: table: 4 (over z_lo), row: 64 (over z_hi, y, x, core).
Axes of the slice: x: 4, y: 4, z: 8 (z_hi: 2, z_lo: 4; z = z_hi * 4 + z_lo), core: 2. Of those that a mesh axis runs over, the one named last changes fastest.
Arguments:
- tables: bfloat16 [4, 524288, 128], P('table', 'row'), may hold values from -3 to 3
- indices: int32 [4, 100, 512], P('table'), may hold values from 0 to 524287
- weights: bfloat16 [4, 100, 512], P('table'), may hold values from 0.19921875 to 1
- lengths: int32 [4, 512], P('table'), may hold values from 1 to 100, as said below
Outputs:
- pooled: bfloat16 [4, 512, 128], P(None, ('table', 'row'))
Inputs may be any that keep to these rules, and one draw needn't show every extreme that they name: `lengths`: the longest bag of each table has a power of two of at most 64 positions, or 100 positions, and some table has a bag of 100.
All inputs are finite; a program needn't handle non-finite values.
Results may differ from a plain program's by a relative error of at most 0.001.
Values may be sent and summed in bfloat16 or wider, within the bound.
No kernel may reach another device: no remote copies, remote signals or barrier semaphores. Data moves between devices by JAX's collectives and lax.ppermute only.
A program may use at most 64 MiB of HBM per device.

v0:
```python
import jax
import jax.numpy as jnp
from jax import lax
from jax.experimental import pallas as pl
from jax.experimental.pallas import tpu as pltpu
from jax.sharding import Mesh
from jax.sharding import PartitionSpec as P

lanes = 128
packed_rows = 16
slots = 16
weight_unit = 1024
vmem_bytes = 20 * 2**20


def read_positions(start_ref, index_ref, weight_ref, length_ref, rank_ref, code_ref, rows):
    bag, _, batch = index_ref.shape
    padded = rank_ref.shape[0]
    local = index_ref[:, 0, :] - start_ref[0]
    position = lax.broadcasted_iota(jnp.int32, (bag, batch), 0)
    inside = (local >= 0) & (local < rows) & (position < length_ref[...])
    code = local.astype(jnp.float32) * (2.0 * weight_unit)
    code = code + weight_ref[...].astype(jnp.float32) * weight_unit
    code_ref[:bag, :] = jnp.where(inside, code, 0.0)
    code_ref[bag:, :] = jnp.zeros((padded - bag, batch), jnp.float32)

    used = jnp.where(inside, 1.0, 0.0)
    used = jnp.concatenate([used, jnp.zeros((lanes - bag, batch), jnp.float32)], 0)
    before = lax.broadcasted_iota(jnp.int32, (padded, lanes), 0) > lax.broadcasted_iota(
        jnp.int32, (padded, lanes), 1
    )
    rank = jnp.dot(
        jnp.where(before, 1.0, 0.0).astype(jnp.bfloat16),
        used.astype(jnp.bfloat16),
        preferred_element_type=jnp.float32,
    )
    rank_ref[...] = rank
    return jnp.max(rank[padded - 1 :, :], keepdims=True)


def rounds_for(most):
    return (jnp.max(most).astype(jnp.int32) + (slots - 1)) // slots


def fill_slots(rank_ref, code_ref, slot_refs, first):
    high_ref, low_ref, factor_ref = slot_refs
    groups = high_ref.shape[0]
    planes = []
    for block in range(rank_ref.shape[1] // lanes):
        where = pl.ds(block * lanes, lanes)
        rank = rank_ref[:, where]
        code = code_ref[:, where]
        for s in range(slots):
            at = rank == (first + s).astype(jnp.float32)
            planes.append(jnp.sum(jnp.where(at, code, 0.0), axis=0, keepdims=True))
    plane = jnp.concatenate(planes, 0)
    plane = jnp.concatenate([plane, pltpu.roll(plane, lanes - groups, 1)], 0)
    code = plane.T[:groups].astype(jnp.int32)
    row = code // (2 * weight_unit)
    high_ref[...] = (row // lanes).astype(jnp.float32)
    low_ref[...] = (row % lanes).astype(jnp.float32)
    factor = (code % (2 * weight_unit)).astype(jnp.float32)
    factor_ref[...] = factor * (1.0 / weight_unit)


def spread_half(slot_refs, spread_ref, core, tiles, inexact, add):
    high_ref, low_ref, factor_ref = slot_refs
    group_bags = lanes // slots
    half_groups = high_ref.shape[0] // 2
    stride = spread_ref.shape[0] // tiles
    row_id = lax.broadcasted_iota(jnp.int32, (packed_rows, lanes), 0)
    row_ids = [
        (row_id + packed_rows * i).astype(jnp.float32).astype(jnp.bfloat16)
        for i in range(lanes // packed_rows)
    ]
    zero = jnp.zeros((packed_rows, lanes), jnp.bfloat16)
    one = jnp.ones((packed_rows, lanes), jnp.bfloat16)
    owner = lax.broadcasted_iota(jnp.int32, (packed_rows, lanes), 1) // slots
    owner = owner.astype(jnp.float32).astype(jnp.bfloat16)
    owned = [owner == jnp.full_like(owner, g) for g in range(group_bags)]
    inexact = list(inexact)

    def row_of(ref, j):
        row = ref[pl.ds(j, 1), :]
        return jnp.broadcast_to(row, (packed_rows, lanes)).astype(jnp.bfloat16)

    for t in range(half_groups):
        j = t // 2 * 4 + t % 2 + 2 * core
        high = row_of(high_ref, j)
        low = row_of(low_ref, j)
        factor = row_of(factor_ref, j)
        at = [high == ids for ids in row_ids[: tiles // packed_rows]]
        by_high = []
        for g in range(group_bags):
            mine = jnp.where(owned[g], factor, zero)
            by_high += [jnp.where(hit, mine, zero) for hit in at]
        by_low = [jnp.where(low == ids, one, zero) for ids in row_ids]
        total = lax.dot_general(
            jnp.concatenate(by_high, 0),
            jnp.concatenate(by_low, 0),
            (((1,), (1,)), ((), ())),
            preferred_element_type=jnp.float32,
        )
        blocks = group_bags // 2
        for g in range(group_bags):
            first = (g % blocks * 2 + g // blocks) * half_groups
            where = pl.ds(first + t, tiles, stride=stride)
            part = total[g * tiles : (g + 1) * tiles]
            if add:
                part = part + spread_ref[where, :]
            spread_ref[where, :] = part
            rest = jnp.abs(part - part.astype(jnp.bfloat16).astype(jnp.float32))
            for o in range(len(inexact)):
                inexact[o] = jnp.maximum(inexact[o], rest[o * 8 : (o + 1) * 8])
    return tuple(inexact)


def multiply(spread_ref, table_ref, inexact, out_ref):
    tiles = table_ref.shape[0] // lanes
    stride = spread_ref.shape[0] // tiles
    bags = out_ref.shape[0]
    left = [jnp.max(most) for most in inexact]
    factors = [
        spread_ref[pl.ds(i * stride, bags), :].astype(jnp.bfloat16) for i in range(tiles)
    ]
    out_ref[...] = jnp.dot(
        jnp.concatenate(factors, 1), table_ref[...], preferred_element_type=jnp.float32
    )

    for o in range(len(inexact)):

        @pl.when(left[o] > 0)
        def _(o=o):
            factors = jnp.concatenate(
                [spread_ref[pl.ds((8 * o + i) * stride, bags), :] for i in range(8)], 1
            )
            rest = factors - factors.astype(jnp.bfloat16).astype(jnp.float32)
            out_ref[...] += jnp.dot(
                rest.astype(jnp.bfloat16),
                table_ref[pl.ds(8 * o * lanes, 8 * lanes), :],
                preferred_element_type=jnp.float32,
            )


def exact_so_far(tiles):
    return tuple(jnp.zeros((8, lanes), jnp.float32) for _ in range(tiles // 8))


def send_kernel(
    start_ref,
    core_ref,
    index_hbm,
    weight_hbm,
    length_hbm,
    table_hbm,
    out_ref,
    high_ref,
    low_ref,
    factor_ref,
    most_ref,
    table_ref,
    index_ref,
    weight_ref,
    length_ref,
    rank_ref,
    code_ref,
    high_later,
    low_later,
    factor_later,
    spread_ref,
    table_sem,
    index_sem,
    weight_sem,
    length_sem,
):
    copies = [
        pltpu.make_async_copy(index_hbm, index_ref, index_sem),
        pltpu.make_async_copy(weight_hbm, weight_ref, weight_sem),
        pltpu.make_async_copy(length_hbm, length_ref, length_sem),
    ]
    for copy in copies:
        copy.start()
    for copy in copies:
        copy.wait()
    table_copy = pltpu.make_async_copy(table_hbm, table_ref, table_sem)
    table_copy.start()
    rows = table_ref.shape[0]
    tiles = rows // lanes
    core = 1 - core_ref[0]
    most = read_positions(
        start_ref, index_ref, weight_ref, length_ref, rank_ref, code_ref, rows
    )
    most_ref[...] = jnp.broadcast_to(most, most_ref.shape)
    rounds = rounds_for(most)
    slot_refs = (high_ref, low_ref, factor_ref)
    later_refs = (high_later, low_later, factor_later)
    fill_slots(rank_ref, code_ref, slot_refs, jnp.int32(0))
    inexact = spread_half(slot_refs, spread_ref, core, tiles, exact_so_far(tiles), False)

    def later_round(number, inexact):
        fill_slots(rank_ref, code_ref, later_refs, number * slots)
        return spread_half(later_refs, spread_ref, core, tiles, inexact, True)

    inexact = lax.fori_loop(1, rounds, later_round, inexact)
    table_copy.wait()
    multiply(spread_ref, table_ref, inexact, out_ref)


def keep_kernel(
    start_ref,
    core_ref,
    most_ref,
    high_ref,
    low_ref,
    factor_ref,
    index_hbm,
    weight_hbm,
    length_hbm,
    table_hbm,
    out_ref,
    table_ref,
    index_ref,
    weight_ref,
    length_ref,
    rank_ref,
    code_ref,
    high_later,
    low_later,
    factor_later,
    spread_ref,
    table_sem,
    index_sem,
    weight_sem,
    length_sem,
):
    table_copy = pltpu.make_async_copy(table_hbm, table_ref, table_sem)
    table_copy.start()
    rows = table_ref.shape[0]
    tiles = rows // lanes
    core = core_ref[0]
    slot_refs = (high_ref, low_ref, factor_ref)
    later_refs = (high_later, low_later, factor_later)
    inexact = spread_half(slot_refs, spread_ref, core, tiles, exact_so_far(tiles), False)
    rounds = rounds_for(most_ref[...])

    @pl.when(rounds > 1)
    def _():
        copies = [
            pltpu.make_async_copy(index_hbm, index_ref, index_sem),
            pltpu.make_async_copy(weight_hbm, weight_ref, weight_sem),
            pltpu.make_async_copy(length_hbm, length_ref, length_sem),
        ]
        for copy in copies:
            copy.start()
        for copy in copies:
            copy.wait()
        read_positions(start_ref, index_ref, weight_ref, length_ref, rank_ref, code_ref, rows)

    def later_round(number, inexact):
        fill_slots(rank_ref, code_ref, later_refs, number * slots)
        return spread_half(later_refs, spread_ref, core, tiles, inexact, True)

    inexact = lax.fori_loop(1, rounds, later_round, inexact)
    table_copy.wait()
    multiply(spread_ref, table_ref, inexact, out_ref)


def kernels(table_rows, index_rows, weight, length, row_start, core):
    rows, width = table_rows.shape
    bag, batch = weight.shape
    padded = bag + 8 - bag % 8
    groups = batch * slots // lanes
    half = batch // 2
    tiles = rows // lanes
    smem = pl.BlockSpec(memory_space=pltpu.SMEM)
    vmem = pl.BlockSpec(memory_space=pltpu.VMEM)
    far = pl.BlockSpec(memory_space=pl.ANY)
    table_scratch = pltpu.VMEM((rows, width), table_rows.dtype)
    by_position = [pltpu.VMEM((padded, batch), jnp.float32)] * 2
    by_group = [pltpu.VMEM((groups, lanes), jnp.float32)] * 3
    spread = pltpu.VMEM(((half + 1) * tiles, lanes), jnp.float32)
    dma = pltpu.SemaphoreType.DMA
    scratch = [
        table_scratch,
        pltpu.VMEM(index_rows.shape, index_rows.dtype),
        pltpu.VMEM(weight.shape, weight.dtype),
        pltpu.VMEM(length.shape, length.dtype),
        *by_position,
        *by_group,
        spread,
        dma,
        dma,
        dma,
        dma,
    ]
    limit = pltpu.CompilerParams(vmem_limit_bytes=vmem_bytes)
    index_rows, weight, length, table_rows = [
        pltpu.with_memory_space_constraint(value, pltpu.HBM)
        for value in (index_rows, weight, length, table_rows)
    ]
    pools = jax.ShapeDtypeStruct((half, width), jnp.float32)
    slot = jax.ShapeDtypeStruct((groups, lanes), jnp.float32)
    place = (row_start.reshape(1), core.reshape(1))

    sent, high, low, factor, most = pl.pallas_call(
        send_kernel,
        out_shape=(pools, slot, slot, slot, jax.ShapeDtypeStruct((8, lanes), jnp.float32)),
        in_specs=[smem, smem, far, far, far, far],
        out_specs=(vmem, vmem, vmem, vmem, vmem),
        scratch_shapes=scratch,
        compiler_params=limit,
    )(*place, index_rows, weight, length, table_rows)

    def keep():
        return pl.pallas_call(
            keep_kernel,
            out_shape=pools,
            in_specs=[smem, smem, vmem, vmem, vmem, vmem, far, far, far, far],
            out_specs=vmem,
            scratch_shapes=scratch,
            compiler_params=limit,
            cost_estimate=pl.CostEstimate(
                flops=8 * half * rows * width, bytes_accessed=rows * width * 2, transcendentals=0
            ),
        )(*place, most, high, low, factor, index_rows, weight, length, table_rows)

    return sent, keep


def on_device(tables, indices, weights, lengths):
    _, row_dev, feature_width = tables.shape
    batch_size = indices.shape[2]
    table_count = lax.axis_size("table")
    pair_count = lax.axis_size("pair")
    core = lax.axis_index("core").astype(jnp.int32)
    row = lax.axis_index("pair").astype(jnp.int32) * 2 + core
    index_rows = indices.transpose(1, 0, 2)
    sent, keep = kernels(tables[0], index_rows, weights[0], lengths, row * row_dev, core)
    received = lax.ppermute(sent, "core", [(0, 1), (1, 0)])
    partial = keep() + received
    share = batch_size // (table_count * pair_count * 2)
    tiles = partial.reshape(table_count * pair_count, share, feature_width)
    arrived = lax.all_to_all(tiles, ("table", "pair"), split_axis=0, concat_axis=0, tiled=True)
    shares = arrived.reshape(table_count, pair_count, share, feature_width)
    return shares.sum(axis=1).astype(jnp.bfloat16)


def solution(mesh):
    tables, rows = mesh.devices.shape
    by_core = Mesh(mesh.devices.reshape(tables, rows // 2, 2), ("table", "pair", "core"))
    row = ("pair", "core")
    placed = (
        P("table", row, None),
        P("table", None, None),
        P("table", None, None),
        P("table", None),
    )
    return jax.shard_map(
        on_device,
        mesh=by_core,
        in_specs=placed,
        out_specs=P(None, ("table", *row), None),
        check_vma=False,
    )
```

profile of v0, /device:TPU:1, one launch (start us, length us, event | category | flops | bytes accessed | tf_op | source)
XLA Modules:
  0.0 36.8 jit_solution(5407700211567013753)
XLA Ops:
  0.0 4.9 %shard_map.46 = (f32[256,128]{1,0:T(8,128)S(1)}, f32[64,128]{1,0:T(8,128)S(1)}, f32[64,128]{1,0:T(8,128)S(1)}, f32[64,128]{1,0:T(8,128)S(1)}, f32[8,128]{1,0:T(8,128)S(1)}) custom-call(s32[1]{0:T(128)} %bitcast.start_ref, s32[1]{0:T(128)} %bitcast.1.core_ref, s32[100,1,512]{2,1,0:T(1,128)} %bitcast.11, bf16[100,512]{1,0:T(8,128)(2,1)} %bitcast.13, ...), custom_call_target="tpu_custom_call" | custom-call | tf_op jit(solution)/shard_map/pallas_call | solution.py:305
  4.9 3.3 %collective-permute-start = (f32[256,128]{1,0:T(8,128)S(1)}, f32[256,128]{1,0:T(8,128)S(1)}, u32[]{:S(2)}, u32[]{:S(2)}) collective-permute-start(f32[256,128]{1,0:T(8,128)S(1)} %get-tuple-element.14), channel_id=1, source_target_pairs={{0,1},{1,0},{2,3},{3,2},{4,5},{5,4},{6,7},{7,6},{8,9},{9,8},{10,11... | collective-permute-start | bytes 393224 | tf_op jit(solution)/shard_map/ppermute | solution.py:339
  8.2 3.2 %shard_map.47 = f32[256,128]{1,0:T(8,128)S(1)} custom-call(s32[1]{0:T(128)} %bitcast.start_ref, s32[1]{0:T(128)} %bitcast.1.core_ref, f32[8,128]{1,0:T(8,128)S(1)} %get-tuple-element.10.most_ref, f32[64,128]{1,0:T(8,128)S(1)} %get-tuple-element.11.high_ref, f32[64,128]{1,0:T(8,128)S(1)} %get-tuple-element.12.low_ref, ...), custom_call_target="tpu_custom_call" | custom-call | flops 2147483648 | bytes 2097152 | tf_op jit(solution)/shard_map/pallas_call | solution.py:315
  11.5 0.0 collective-permute-done
  11.5 24.7 %all_to_all.5 = f32[128,2,128]{2,1,0:T(2,128)S(1)} all-to-all(f32[128,2,128]{2,1,0:T(2,128)S(1)} %bitcast.10), channel_id=1, replica_groups=mesh['table'=4,'pair'=32,'core'=2] {'table','pair'}, dimensions={0} | all-to-all | bytes 262144 | tf_op jit(solution)/shard_map/all_to_all | solution.py:343
  36.2 0.6 %bitcast_reduce_fusion = bf16[4,2,128]{2,1,0:T(2,128)(2,1)} fusion(f32[128,2,128]{2,1,0:T(2,128)S(1)} %all_to_all.5), kind=kLoop, calls=%fused_computation | loop fusion | flops 31744 | bytes 133120 | tf_op jit(solution)/shard_map/reduce_sum | solution.py:345
  (1 shorter events, 0.0 us)
Async XLA Ops:
  4.9 6.5 %collective-permute-start = (f32[256,128]{1,0:T(8,128)S(1)}, f32[256,128]{1,0:T(8,128)S(1)}, u32[]{:S(2)}, u32[]{:S(2)}) collective-permute-start(f32[256,128]{1,0:T(8,128)S(1)} %get-tuple-element.14), channel_id=1, source_target_pairs={{0,1},{1,0},{2,3},{3,2},{4,5},{5,4},{6,7},{7,6},{8,9},{9,8},{10,11... | collective-permute-start | bytes 393224 | tf_op jit(solution)/shard_map/ppermute | solution.py:339
where the time goes:
time: 37.3 us; the launch traced here: 36.8 us
  blocking collectives  24.7 us (66%)
  Pallas kernels  8.15 us (22%)
  starting transfers between devices  3.29 us (9%)
  other arithmetic  0.64 us (2%)
    all_to_all x1, blocking collectives, on_device(): lax.all_to_all(tiles, ('table', 'pair'), split_axis=0, concat_axis=0, til...  24.7 us
    pallas_call x1, Pallas kernels, kernels(): pl.pallas_call(send_kernel, out_shape=(pools, slot, slot, slot, jax.Shape...  4.91 us
    ppermute x1, starting transfers between devices, on_device(): received = lax.ppermute(sent, 'core', [(0, 1), (1, 0)])  3.29 us
    pallas_call x1, Pallas kernels, keep(): pl.pallas_call(keep_kernel, out_shape=pools, in_specs=[smem, smem, vmem,...  3.24 us
  transfers between devices with their start and end apart: 1, of which 0 were waited for; matrix products, arithmetic and copies ran while one was open for 0% of the time, Pallas kernels for 9%

commit v1 on v0

--- a/solution.py
+++ b/solution.py
@@ -1,3 +1,5 @@
+import functools
+
 import jax
 import jax.numpy as jnp
 from jax import lax
@@ -42,7 +44,25 @@
     return (jnp.max(most).astype(jnp.int32) + (slots - 1)) // slots
 
 
-def fill_slots(rank_ref, code_ref, slot_refs, first):
+def note_repeats(plane, repeated_ref):
+    row = (plane.astype(jnp.int32) // (2 * weight_unit)).astype(jnp.float32)
+    slot = lax.broadcasted_iota(jnp.int32, plane.shape, 0).astype(jnp.float32)
+    row = jnp.where(plane > 0, row, -1.0 - slot)
+    noted = []
+    for first in range(0, plane.shape[0], slots):
+        rows = row[first : first + slots]
+        again = jnp.full(rows.shape, -1.0, jnp.float32)
+        for shift in range(1, slots // 2 + 1):
+            again = jnp.where(rows == pltpu.roll(rows, shift, 0), rows, again)
+        noted.append((again.astype(jnp.int32) >> 8).astype(jnp.float32))
+    for pair in range(repeated_ref.shape[0]):
+        hits = functools.reduce(
+            jnp.maximum, [jnp.where(pairs == float(pair), 1.0, 0.0) for pairs in noted]
+        )
+        repeated_ref[pair : pair + 1, :] = jnp.max(hits, axis=0, keepdims=True)
+
+
+def fill_slots(rank_ref, code_ref, slot_refs, first, repeated_ref=None):
     high_ref, low_ref, factor_ref = slot_refs
     groups = high_ref.shape[0]
     planes = []
@@ -54,16 +74,18 @@
             at = rank == (first + s).astype(jnp.float32)
             planes.append(jnp.sum(jnp.where(at, code, 0.0), axis=0, keepdims=True))
     plane = jnp.concatenate(planes, 0)
+    if repeated_ref is not None:
+        note_repeats(plane, repeated_ref)
     plane = jnp.concatenate([plane, pltpu.roll(plane, lanes - groups, 1)], 0)
+    low_ref[...] = (plane.astype(jnp.int32) // (2 * weight_unit) % lanes).astype(jnp.float32)
     code = plane.T[:groups].astype(jnp.int32)
     row = code // (2 * weight_unit)
     high_ref[...] = (row // lanes).astype(jnp.float32)
-    low_ref[...] = (row % lanes).astype(jnp.float32)
     factor = (code % (2 * weight_unit)).astype(jnp.float32)
     factor_ref[...] = factor * (1.0 / weight_unit)
 
 
-def spread_half(slot_refs, spread_ref, core, tiles, inexact, add):
+def spread_half(slot_refs, spread_ref, core, tiles, add):
     high_ref, low_ref, factor_ref = slot_refs
     group_bags = lanes // slots
     half_groups = high_ref.shape[0] // 2
@@ -71,14 +93,14 @@
     row_id = lax.broadcasted_iota(jnp.int32, (packed_rows, lanes), 0)
     row_ids = [
         (row_id + packed_rows * i).astype(jnp.float32).astype(jnp.bfloat16)
-        for i in range(lanes // packed_rows)
+        for i in range(tiles // packed_rows)
     ]
     zero = jnp.zeros((packed_rows, lanes), jnp.bfloat16)
-    one = jnp.ones((packed_rows, lanes), jnp.bfloat16)
+    lane = lax.broadcasted_iota(jnp.int32, (lanes, lanes), 1).astype(jnp.float32)
+    lows = pltpu.roll(low_ref[...], (lanes - 2 * core) % lanes, 1)
     owner = lax.broadcasted_iota(jnp.int32, (packed_rows, lanes), 1) // slots
     owner = owner.astype(jnp.float32).astype(jnp.bfloat16)
     owned = [owner == jnp.full_like(owner, g) for g in range(group_bags)]
-    inexact = list(inexact)
 
     def row_of(ref, j):
         row = ref[pl.ds(j, 1), :]
@@ -87,18 +109,19 @@
     for t in range(half_groups):
         j = t // 2 * 4 + t % 2 + 2 * core
         high = row_of(high_ref, j)
-        low = row_of(low_ref, j)
         factor = row_of(factor_ref, j)
-        at = [high == ids for ids in row_ids[: tiles // packed_rows]]
+        at = [high == ids for ids in row_ids]
         by_high = []
         for g in range(group_bags):
             mine = jnp.where(owned[g], factor, zero)
             by_high += [jnp.where(hit, mine, zero) for hit in at]
-        by_low = [jnp.where(low == ids, one, zero) for ids in row_ids]
+        at_lane = t // 2 * 4 + t % 2
+        low = jnp.broadcast_to(lows[:, at_lane : at_lane + 1], (lanes, lanes))
+        by_low = jnp.where(low == lane, 1.0, 0.0).astype(jnp.bfloat16)
         total = lax.dot_general(
             jnp.concatenate(by_high, 0),
-            jnp.concatenate(by_low, 0),
-            (((1,), (1,)), ((), ())),
+            by_low,
+            (((1,), (0,)), ((), ())),
             preferred_element_type=jnp.float32,
         )
         blocks = group_bags // 2
@@ -109,17 +132,19 @@
             if add:
                 part = part + spread_ref[where, :]
             spread_ref[where, :] = part
-            rest = jnp.abs(part - part.astype(jnp.bfloat16).astype(jnp.float32))
-            for o in range(len(inexact)):
-                inexact[o] = jnp.maximum(inexact[o], rest[o * 8 : (o + 1) * 8])
-    return tuple(inexact)
-
-
-def multiply(spread_ref, table_ref, inexact, out_ref):
+
+
+def multiply(spread_ref, table_ref, repeated_ref, core, rounds, out_ref):
     tiles = table_ref.shape[0] // lanes
     stride = spread_ref.shape[0] // tiles
     bags = out_ref.shape[0]
-    left = [jnp.max(most) for most in inexact]
+    lane = lax.broadcasted_iota(jnp.int32, (1, lanes), 1)
+    ours = (lane // 2) % 2 == core
+    left = [
+        jnp.where(ours, repeated_ref[pair : pair + 1, :], 0.0) for pair in range(tiles // 2)
+    ]
+    any_left = (jnp.max(functools.reduce(jnp.maximum, left)) > 0) | (rounds > 1)
+    left = [(jnp.max(some) > 0) | (rounds > 1) for some in left]
     factors = [
         spread_ref[pl.ds(i * stride, bags), :].astype(jnp.bfloat16) for i in range(tiles)
     ]
@@ -127,23 +152,20 @@
         jnp.concatenate(factors, 1), table_ref[...], preferred_element_type=jnp.float32
     )
 
-    for o in range(len(inexact)):
-
-        @pl.when(left[o] > 0)
-        def _(o=o):
-            factors = jnp.concatenate(
-                [spread_ref[pl.ds((8 * o + i) * stride, bags), :] for i in range(8)], 1
-            )
-            rest = factors - factors.astype(jnp.bfloat16).astype(jnp.float32)
-            out_ref[...] += jnp.dot(
-                rest.astype(jnp.bfloat16),
-                table_ref[pl.ds(8 * o * lanes, 8 * lanes), :],
-                preferred_element_type=jnp.float32,
-            )
-
-
-def exact_so_far(tiles):
-    return tuple(jnp.zeros((8, lanes), jnp.float32) for _ in range(tiles // 8))
+    def add_rest(pair):
+        factors = [spread_ref[pl.ds((2 * pair + i) * stride, bags), :] for i in range(2)]
+        factors = jnp.concatenate(factors, 1)
+        rest = factors - factors.astype(jnp.bfloat16).astype(jnp.float32)
+        out_ref[...] += jnp.dot(
+            rest.astype(jnp.bfloat16),
+            table_ref[pl.ds(2 * pair * lanes, 2 * lanes), :],
+            preferred_element_type=jnp.float32,
+        )
+
+    @pl.when(any_left)
+    def _():
+        for pair in range(tiles // 2):
+            pl.when(left[pair])(functools.partial(add_rest, pair))
 
 
 def send_kernel(
@@ -158,6 +180,7 @@
     low_ref,
     factor_ref,
     most_ref,
+    repeated_ref,
     table_ref,
     index_ref,
     weight_ref,
@@ -194,22 +217,24 @@
     rounds = rounds_for(most)
     slot_refs = (high_ref, low_ref, factor_ref)
     later_refs = (high_later, low_later, factor_later)
-    fill_slots(rank_ref, code_ref, slot_refs, jnp.int32(0))
-    inexact = spread_half(slot_refs, spread_ref, core, tiles, exact_so_far(tiles), False)
-
-    def later_round(number, inexact):
+    fill_slots(rank_ref, code_ref, slot_refs, jnp.int32(0), repeated_ref)
+    spread_half(slot_refs, spread_ref, core, tiles, False)
+
+    def later_round(number, carry):
         fill_slots(rank_ref, code_ref, later_refs, number * slots)
-        return spread_half(later_refs, spread_ref, core, tiles, inexact, True)
-
-    inexact = lax.fori_loop(1, rounds, later_round, inexact)
+        spread_half(later_refs, spread_ref, core, tiles, True)
+        return carry
+
+    lax.fori_loop(1, rounds, later_round, 0)
     table_copy.wait()
-    multiply(spread_ref, table_ref, inexact, out_ref)
+    multiply(spread_ref, table_ref, repeated_ref, core, rounds, out_ref)
 
 
 def keep_kernel(
     start_ref,
     core_ref,
     most_ref,
+    repeated_ref,
     high_ref,
     low_ref,
     factor_ref,
@@ -240,7 +265,7 @@
     core = core_ref[0]
     slot_refs = (high_ref, low_ref, factor_ref)
     later_refs = (high_later, low_later, factor_later)
-    inexact = spread_half(slot_refs, spread_ref, core, tiles, exact_so_far(tiles), False)
+    spread_half(slot_refs, spread_ref, core, tiles, False)
     rounds = rounds_for(most_ref[...])
 
     @pl.when(rounds > 1)
@@ -256,13 +281,14 @@
             copy.wait()
         read_positions(start_ref, index_ref, weight_ref, length_ref, rank_ref, code_ref, rows)
 
-    def later_round(number, inexact):
+    def later_round(number, carry):
         fill_slots(rank_ref, code_ref, later_refs, number * slots)
-        return spread_half(later_refs, spread_ref, core, tiles, inexact, True)
-
-    inexact = lax.fori_loop(1, rounds, later_round, inexact)
+        spread_half(later_refs, spread_ref, core, tiles, True)
+        return carry
+
+    lax.fori_loop(1, rounds, later_round, 0)
     table_copy.wait()
-    multiply(spread_ref, table_ref, inexact, out_ref)
+    multiply(spread_ref, table_ref, repeated_ref, core, rounds, out_ref)
 
 
 def kernels(table_rows, index_rows, weight, length, row_start, core):
@@ -277,7 +303,7 @@
     far = pl.BlockSpec(memory_space=pl.ANY)
     table_scratch = pltpu.VMEM((rows, width), table_rows.dtype)
     by_position = [pltpu.VMEM((padded, batch), jnp.float32)] * 2
-    by_group = [pltpu.VMEM((groups, lanes), jnp.float32)] * 3
+    by_group = [pltpu.VMEM((n, lanes), jnp.float32) for n in (groups, lanes, groups)]
     spread = pltpu.VMEM(((half + 1) * tiles, lanes), jnp.float32)
     dma = pltpu.SemaphoreType.DMA
     scratch = [
@@ -299,14 +325,19 @@
         for value in (index_rows, weight, length, table_rows)
     ]
     pools = jax.ShapeDtypeStruct((half, width), jnp.float32)
-    slot = jax.ShapeDtypeStruct((groups, lanes), jnp.float32)
+    slot = [jax.ShapeDtypeStruct((n, lanes), jnp.float32) for n in (groups, lanes, groups)]
     place = (row_start.reshape(1), core.reshape(1))
 
-    sent, high, low, factor, most = pl.pallas_call(
+    sent, high, low, factor, most, repeated = pl.pallas_call(
         send_kernel,
-        out_shape=(pools, slot, slot, slot, jax.ShapeDtypeStruct((8, lanes), jnp.float32)),
+        out_shape=(
+            pools,
+            *slot,
+            jax.ShapeDtypeStruct((8, lanes), jnp.float32),
+            jax.ShapeDtypeStruct((tiles // 2, lanes), jnp.float32),
+        ),
         in_specs=[smem, smem, far, far, far, far],
-        out_specs=(vmem, vmem, vmem, vmem, vmem),
+        out_specs=(vmem,) * 6,
         scratch_shapes=scratch,
         compiler_params=limit,
     )(*place, index_rows, weight, length, table_rows)
@@ -315,14 +346,14 @@
         return pl.pallas_call(
             keep_kernel,
             out_shape=pools,
-            in_specs=[smem, smem, vmem, vmem, vmem, vmem, far, far, far, far],
+            in_specs=[smem, smem, vmem, vmem, vmem, vmem, vmem, far, far, far, far],
             out_specs=vmem,
             scratch_shapes=scratch,
             compiler_params=limit,
             cost_estimate=pl.CostEstimate(
                 flops=8 * half * rows * width, bytes_accessed=rows * width * 2, transcendentals=0
             ),
-        )(*place, most, high, low, factor, index_rows, weight, length, table_rows)
+        )(*place, most, repeated, high, low, factor, index_rows, weight, length, table_rows)
 
     return sent, keep
 

time: 37.3 us -> 36 us (0.965)
  blocking collectives: 24.7 us -> 24 us
    all_to_all x1, blocking collectives: 24.7 us -> 24 us  [on_device(): lax.all_to_all(tiles, ('table', 'pair'), split_axis=0, concat_axis=0, til...]
where the time goes in v1:
time: 36 us; the launch traced here: 35.9 us
  blocking collectives  24 us (67%)
  Pallas kernels  8.25 us (23%)
  starting transfers between devices  2.96 us (8%)
  other arithmetic  0.64 us (2%)
    all_to_all x1, blocking collectives, on_device(): lax.all_to_all(tiles, ('table', 'pair'), split_axis=0, concat_axis=0, til...  24 us
    pallas_call x1, Pallas kernels, kernels(): pl.pallas_call(send_kernel, out_shape=(pools, *slot, jax.ShapeDtypeStruct...  5.01 us
    pallas_call x1, Pallas kernels, keep(): pl.pallas_call(keep_kernel, out_shape=pools, in_specs=[smem, smem, vmem,...  3.24 us
    ppermute x1, starting transfers between devices, on_device(): received = lax.ppermute(sent, 'core', [(0, 1), (1, 0)])  2.96 us
  transfers between devices with their start and end apart: 1, of which 0 were waited for; matrix products, arithmetic and copies ran while one was open for 0% of the time, Pallas kernels for 9%

profile of v1, /device:TPU:1, one launch (start us, length us, event | category | flops | bytes accessed | tf_op | source)
XLA Modules:
  0.0 35.9 jit_solution(4035856415252407142)
XLA Ops:
  0.0 5.0 %shard_map.46 = (f32[256,128]{1,0:T(8,128)S(1)}, f32[64,128]{1,0:T(8,128)S(1)}, f32[128,128]{1,0:T(8,128)S(1)}, f32[64,128]{1,0:T(8,128)S(1)}, f32[8,128]{1,0:T(8,128)S(1)}, /*index=5*/f32[32,128]{1,0:T(8,128)S(1)}) custom-call(s32[1]{0:T(128)} %bitcast.start_ref, s32[1]{0:T(128)} %bitcast.1.core_ref, s32[100,1,512]{2,1,0:T(1,128)} %bitcast.11, ...), custom_call_target="tpu_custom_call" | custom-call | tf_op jit(solution)/shard_map/pallas_call | solution.py:331
  5.0 3.0 %collective-permute-start = (f32[256,128]{1,0:T(8,128)S(1)}, f32[256,128]{1,0:T(8,128)S(1)}, u32[]{:S(2)}, u32[]{:S(2)}) collective-permute-start(f32[256,128]{1,0:T(8,128)S(1)} %get-tuple-element.16), channel_id=1, source_target_pairs={{0,1},{1,0},{2,3},{3,2},{4,5},{5,4},{6,7},{7,6},{8,9},{9,8},{10,11... | collective-permute-start | bytes 393224 | tf_op jit(solution)/shard_map/ppermute | solution.py:370
  8.0 3.2 %shard_map.47 = f32[256,128]{1,0:T(8,128)S(1)} custom-call(s32[1]{0:T(128)} %bitcast.start_ref, s32[1]{0:T(128)} %bitcast.1.core_ref, f32[8,128]{1,0:T(8,128)S(1)} %get-tuple-element.11.most_ref, f32[32,128]{1,0:T(8,128)S(1)} %get-tuple-element.12.repeated_ref, f32[64,128]{1,0:T(8,128)S(1)} %get-tuple-element.13.high_ref, ...), custom_call_target="tpu_custom_call" | custom-call | flops 2147483648 | bytes 2097152 | tf_op jit(solution)/shard_map/pallas_call | solution.py:346
  11.2 0.0 collective-permute-done
  11.3 24.0 %all_to_all.5 = f32[128,2,128]{2,1,0:T(2,128)S(1)} all-to-all(f32[128,2,128]{2,1,0:T(2,128)S(1)} %bitcast.10), channel_id=1, replica_groups=mesh['table'=4,'pair'=32,'core'=2] {'table','pair'}, dimensions={0} | all-to-all | bytes 262144 | tf_op jit(solution)/shard_map/all_to_all | solution.py:374
  35.3 0.6 %bitcast_reduce_fusion = bf16[4,2,128]{2,1,0:T(2,128)(2,1)} fusion(f32[128,2,128]{2,1,0:T(2,128)S(1)} %all_to_all.5), kind=kLoop, calls=%fused_computation | loop fusion | flops 31744 | bytes 133120 | tf_op jit(solution)/shard_map/reduce_sum | solution.py:376
  (1 shorter events, 0.0 us)
Async XLA Ops:
  5.0 6.2 %collective-permute-start = (f32[256,128]{1,0:T(8,128)S(1)}, f32[256,128]{1,0:T(8,128)S(1)}, u32[]{:S(2)}, u32[]{:S(2)}) collective-permute-start(f32[256,128]{1,0:T(8,128)S(1)} %get-tuple-element.16), channel_id=1, source_target_pairs={{0,1},{1,0},{2,3},{3,2},{4,5},{5,4},{6,7},{7,6},{8,9},{9,8},{10,11... | collective-permute-start | bytes 393224 | tf_op jit(solution)/shard_map/ppermute | solution.py:370
